TPU v7x, 128 devices: a whole 4x4x4 slice. The times are simulated.
128 devices in a mesh: ga: 16 (over x, z_hi, core), ba: 8 (over y, z_lo).
Axes of the slice: x: 4, y: 4, z: 4 (z_hi: 2, z_lo: 2; z = z_hi * 2 + z_lo), core: 2. Of those that a mesh axis runs over, the one named last changes fastest.
Arguments:
- psi: float32 [2, 32768, 2048], P(None, 'ga', 'ba'), may hold values from -0.15625 to 0.15625
- dpsi: float32 [2, 32768, 512], P(None, 'ga', 'ba'), may hold values from -6 to 6
- band_weight: float32 [2048], replicated, may hold values from 0.25 to 1
- panel_band: int32 [16], P('ba'), may hold values from 0 to 15, each once
- slab_offset: int32 [16], replicated, may hold values from 0 to 2047
Outputs:
- projected: float32 [2, 32768, 512], P(None, 'ga', 'ba')
Inputs may be any that keep to these rules, and one draw needn't show every extreme that they name: panel_band is a permutation of the panel numbers.
All inputs are finite; a program needn't handle non-finite values.
Results may differ from a plain program's by a relative error of at most 0.00012.
Values sent between devices are 32-bit elements; how exact they have to be, the bound alone decides.
A program may use at most 128 MiB of HBM per device.

v0:
```python
import jax
import jax.numpy as jnp
from jax import lax
from jax.sharding import PartitionSpec as P

PANEL = 128


def split_up(value, dim, count):
    before, after = (value.shape[:dim], value.shape[dim + 1 :])
    return jnp.moveaxis(value.reshape(*before, count, -1, *after), dim, 0)


def edges_of(length, count):
    turn = length // count
    if turn >= 8:
        turn -= turn % 8
    return [turn * k for k in range(1, count)]


def in_order(blocks, dim):
    lengths = list(blocks.shape[1:])
    lengths[dim] *= blocks.shape[0]
    return jnp.moveaxis(blocks, 0, dim).reshape(lengths)


def cut_exchange(value, axis, pieces, split_dim, concat_dim):
    blocks = split_up(value, split_dim, lax.axis_size(axis))
    split_at = max(range(1, max(2, blocks.ndim - 1)), key=lambda d: blocks.shape[d])
    done = []
    for slab in jnp.split(blocks, edges_of(blocks.shape[split_at], pieces), axis=split_at):
        if slab.size:
            done.append(lax.all_to_all(slab, axis, split_axis=0, concat_axis=0, tiled=True))
    return in_order(jnp.concatenate(done, axis=split_at), concat_dim)


def from_everyone(value, axis):
    count = lax.axis_size(axis)
    return lax.all_to_all(
        jnp.broadcast_to(value[None], (count, *value.shape)), axis, 0, 0, tiled=True
    )


def gather_directly(value, axis, dim):
    blocks = from_everyone(value, axis)
    return in_order(blocks, dim)


def tdot(left, right):
    return lax.dot_general(
        left,
        right,
        (((0,), (0,)), ((), ())),
        precision=lax.Precision.HIGHEST,
        preferred_element_type=jnp.float32,
    )


def mdot(left, right):
    return jnp.dot(left, right, precision=lax.Precision.HIGHEST, preferred_element_type=jnp.float32)


def margin_of(waves, columns):
    over_re = tdot(waves[0], columns[0]) + tdot(waves[1], columns[1])
    over_im = tdot(waves[0], columns[1]) - tdot(waves[1], columns[0])
    return jnp.stack([over_re, over_im])


def correct_with(waves, weighted):
    corr_re = mdot(waves[0], weighted[0]) - mdot(waves[1], weighted[1])
    corr_im = mdot(waves[0], weighted[1]) + mdot(waves[1], weighted[0])
    return jnp.stack([corr_re, corr_im])


def weights_for(band_weight, panels):
    table = band_weight.reshape(-1, PANEL)
    onehot = (panels[:, None] == jnp.arange(table.shape[0], dtype=jnp.int32)[None, :]).astype(
        jnp.float32
    )
    return mdot(onehot, table).reshape(-1)


def per_device(psi, dpsi, band_weight, panel_band, slab_offset):
    offset = slab_offset[lax.axis_index("ga")]
    aligned = jnp.roll(dpsi, -offset, axis=1)
    row_waves, row_columns = (
        cut_exchange(psi, "ba", 2, 1, 2),
        cut_exchange(aligned, "ba", 2, 1, 2),
    )
    all_panels = gather_directly(panel_band, "ba", 0)
    full_weight = weights_for(band_weight, all_panels)
    margin = lax.psum(margin_of(row_waves, row_columns), ("ga", "ba"))
    weighted = margin * full_weight[None, :, None]
    row_result = row_columns - correct_with(row_waves, weighted)
    result = lax.all_to_all(row_result, "ba", split_axis=2, concat_axis=1, tiled=True)
    return jnp.roll(result, offset, axis=1)


def solution(mesh):
    in_specs = (P(None, "ga", "ba"), P(None, "ga", "ba"), P(), P("ba"), P())
    out_specs = P(None, "ga", "ba")
    return jax.shard_map(
        per_device, mesh=mesh, in_specs=in_specs, out_specs=out_specs, check_vma=False
    )
```

profile of v0, /device:TPU:2, one launch (start us, length us, event | category | flops | bytes accessed | tf_op | source)
XLA Modules:
  0.0 354.8 jit_solution(3534208202760883374)
XLA Ops:
  6.5 0.0 copy-start
  6.5 1.2 dynamic_slice.6
  8.9 1.8 fusion.9
  10.8 0.3 copy.34
  11.1 0.1 fusion.15
  11.2 0.9 copy.21
  12.1 5.8 %all-to-all-start.1 = ((f32[8,2,128,64]{2,3,1,0:T(8,128)}), f32[8,2,128,64]{2,3,1,0:T(8,128)S(1)}, u32[]{:S(2)}, u32[]{:S(2)}) async-start(f32[8,2,128,64]{2,3,1,0:T(8,128)} %copy.21), calls=%async_computation.1 | async-start | bytes 1048576 | tf_op jit(solution)/shard_map/all_to_all | solution.py:33
  17.9 0.9 copy.20
  18.8 8.7 %all-to-all-done.1 = f32[8,2,128,64]{2,3,1,0:T(8,128)S(1)} async-done(((f32[8,2,128,64]{2,3,1,0:T(8,128)}), f32[8,2,128,64]{2,3,1,0:T(8,128)S(1)}, u32[]{:S(2)}, u32[]{:S(2)}) %all-to-all-start.1) | async-done | bytes 524320 | tf_op jit(solution)/shard_map/all_to_all | solution.py:33
  27.5 3.5 all-to-all-start
  31.0 4.0 %fusion.13 = (f32[8,2,128,256]{3,2,0,1:T(8,128)}, f32[8,2,128,256]{3,2,0,1:T(8,128)S(1)}) fusion(f32[8,2,256,256]{3,2,0,1:T(8,128)} %bitcast.83), kind=kLoop, calls=%fused_computation.29 | loop fusion | bytes 8388608 | tf_op jit(solution)/shard_map/split | solution.py:31
  34.9 1.6 copy.25
  36.5 3.4 all-to-all-done
  39.9 3.6 %all-to-all-start.3 = ((f32[8,2,128,256]{3,2,1,0:T(8,128)}), f32[8,2,128,256]{3,2,1,0:T(8,128)S(1)}, u32[]{:S(2)}, u32[]{:S(2)}) async-start(f32[8,2,128,256]{3,2,1,0:T(8,128)} %copy.25), calls=%async_computation.3 | async-start | bytes 4194304 | tf_op jit(solution)/shard_map/all_to_all | solution.py:33
  43.5 3.1 copy.24
  46.6 26.9 %all-to-all-done.3 = f32[8,2,128,256]{3,2,1,0:T(8,128)S(1)} async-done(((f32[8,2,128,256]{3,2,1,0:T(8,128)}), f32[8,2,128,256]{3,2,1,0:T(8,128)S(1)}, u32[]{:S(2)}, u32[]{:S(2)}) %all-to-all-start.3) | async-done | bytes 2097184 | tf_op jit(solution)/shard_map/all_to_all | solution.py:33
  73.5 4.3 %all-to-all-start.2 = ((f32[8,2,128,256]{3,2,1,0:T(8,128)}), f32[8,2,128,256]{3,2,1,0:T(8,128)}, u32[]{:S(2)}, u32[]{:S(2)}) async-start(f32[8,2,128,256]{3,2,1,0:T(8,128)} %copy.24), calls=%async_computation.2 | async-start | bytes 4194304 | tf_op jit(solution)/shard_map/all_to_all | solution.py:33
  77.8 0.0 all-reduce.2.cloned.1.call-start
  77.9 1.1 copy_bitcast_fusion
  79.0 0.1 fusion.14
  79.1 1.9 copy.27
  81.0 0.0 copy-start.3
  81.0 26.4 %all-to-all-done.2 = f32[8,2,128,256]{3,2,1,0:T(8,128)} async-done(((f32[8,2,128,256]{3,2,1,0:T(8,128)}), f32[8,2,128,256]{3,2,1,0:T(8,128)}, u32[]{:S(2)}, u32[]{:S(2)}) %all-to-all-start.2) | async-done | bytes 2097184 | tf_op jit(solution)/shard_map/all_to_all | solution.py:33
  107.4 3.3 copy.26
  110.7 0.0 copy-done.3
  110.7 2.1 maximum_bitcast_fusion
  112.8 0.4 fusion.12
  113.2 0.0 copy-start.1
  113.2 3.7 %fusion.17 = f32[2048,512]{1,0:T(8,128)S(1)} fusion(f32[256,2048]{0,1:T(8,128)S(1)} %bitcast.68, f32[256,512]{0,1:T(8,128)S(1)} %bitcast.76), kind=kOutput, calls=%fused_computation.33 | convolution fusion | flops 3221225472 | bytes 6815744 | tf_op jit(solution)/shard_map/dot_general | solution.py:50
  116.9 3.7 %fusion.16 = f32[2048,512]{1,0:T(8,128)S(1)} fusion(f32[256,2048]{0,1:T(8,128)S(1)} %bitcast.69, f32[256,512]{0,1:T(8,128)S(1)} %bitcast.78), kind=kOutput, calls=%fused_computation.32 | convolution fusion | flops 3221225472 | bytes 6815744 | tf_op jit(solution)/shard_map/dot_general | solution.py:50
  120.7 3.8 %subtract_bitcast_fusion = f32[1,2048,512]{2,1,0:T(8,128)S(1)} fusion(f32[2048,512]{1,0:T(8,128)S(1)} %fusion.17, f32[256,2048]{0,1:T(8,128)S(1)} %bitcast.72, f32[256,512]{0,1:T(8,128)S(1)} %bitcast.79), kind=kOutput, calls=%fused_computation.5 | convolution fusion | flops 3222274048 | bytes 11010048 | tf_op jit(solution)/shard_map/dot_general | solution.py:50
  124.4 0.0 copy-done.1
  124.4 15.3 %add_bitcast_fusion = f32[1,2048,512]{2,1,0:T(8,128)S(1)} fusion(f32[2048,512]{1,0:T(8,128)S(1)} %fusion.16, f32[256,2048]{0,1:T(8,128)S(1)} %bitcast.73, f32[256,512]{0,1:T(8,128)S(1)} %bitcast.77), kind=kOutput, calls=%fused_computation.6 | convolution fusion | flops 3222274048 | bytes 11010048 | tf_op jit(solution)/shard_map/dot_general | solution.py:50
  139.7 4.2 %pad_maximum_fusion = f32[2,2048,512]{2,1,0:T(8,128)} fusion(f32[1,2048,512]{2,1,0:T(8,128)S(1)} %subtract_bitcast_fusion, f32[1,2048,512]{2,1,0:T(8,128)S(1)} %add_bitcast_fusion), kind=kLoop, calls=%fused_computation | loop fusion | flops 2097152 | bytes 16777216 | tf_op jit(solution)/shard_map/stack | solution.py:66
  143.9 0.0 copy-start.6
  143.9 0.0 copy-start.4
  143.9 0.0 all-reduce.2.cloned.1.call-update
  144.0 0.6 copy-done.6
  144.6 8.5 %all_to_all.44 = s32[8,1,2]{2,1,0:T(1,128)S(1)} all-to-all(s32[8,1,2]{2,1,0:T(1,128)S(1)} %broadcast_in_dim.2), channel_id=1, replica_groups=mesh['ga'=16,'ba'=8] {'ba'}, dimensions={0} | all-to-all | bytes 128 | tf_op jit(solution)/shard_map/all_to_all | solution.py:39
  153.1 0.6 broadcast.7
  153.7 0.7 reduce.3
  154.4 0.1 eq.17
  154.5 0.0 copy-done
  154.5 0.2 convolution_bitcast_fusion
  154.7 0.0 copy-done.4
  154.7 1.3 copy.28
  156.0 148.4 %all-reduce.2.cloned.1.call-done = f32[2,2048,512]{2,1,0:T(8,128)} async-done(((f32[2,2048,512]{2,1,0:T(8,128)}), f32[2,2048,512]{2,1,0:T(8,128)}) %all-reduce.2.cloned.1.call-update) | async-done | bytes 8388624 | tf_op jit(solution)/shard_map/psum | solution.py:92
  304.4 0.0 copy-start.2
  304.4 4.1 %broadcast_multiply_fusion = f32[2,2048,512]{2,1,0:T(8,128)S(1)} fusion(f32[2,2048,512]{2,1,0:T(8,128)} %all-reduce.2.cloned.1.call-done, f32[2048]{0:T(1024)S(1)} %convolution_bitcast_fusion), kind=kLoop, calls=%fused_computation.4 | loop fusion | flops 2097152 | bytes 16785408 | tf_op jit(solution)/shard_map/mul | solution.py:93
  308.6 0.0 copy-done.2
  308.6 3.8 %fusion = f32[256,512]{1,0:T(8,128)S(1)} fusion(f32[256,2048]{0,1:T(8,128)S(1)} %bitcast.74, f32[2,2048,512]{2,1,0:T(8,128)S(1)} %broadcast_multiply_fusion), kind=kOutput, calls=%fused_computation.7 | convolution fusion | flops 3221225472 | bytes 6815744 | tf_op jit(solution)/shard_map/dot_general | solution.py:60
  312.4 3.9 %fusion.1 = f32[256,512]{1,0:T(8,128)S(1)} fusion(f32[256,2048]{0,1:T(8,128)S(1)} %bitcast.70, f32[2,2048,512]{2,1,0:T(8,128)S(1)} %broadcast_multiply_fusion), kind=kOutput, calls=%fused_computation.8 | convolution fusion | flops 3221225472 | bytes 6815744 | tf_op jit(solution)/shard_map/dot_general | solution.py:60
  316.3 4.1 %fusion.7 = f32[1,256,512]{2,1,0:T(8,128)S(1)} fusion(f32[256,512]{1,0:T(8,128)S(1)} %fusion, f32[256,2048]{0,1:T(8,128)S(1)} %bitcast.71, f32[2,2048,512]{2,1,0:T(8,128)S(1)} %broadcast_multiply_fusion), kind=kOutput, calls=%fused_computation.18 | convolution fusion | flops 3221356544 | bytes 7340032 | tf_op jit(solution)/shard_map/dot_general | solution.py:60
  320.3 0.0 copy-start.5
  320.4 3.8 %fusion.5 = f32[1,256,512]{2,1,0:T(8,128)S(1)} fusion(f32[256,512]{1,0:T(8,128)S(1)} %fusion.1, f32[256,2048]{0,1:T(8,128)S(1)} %bitcast.75, f32[2,2048,512]{2,1,0:T(8,128)S(1)} %broadcast_multiply_fusion), kind=kOutput, calls=%fused_computation.16 | convolution fusion | flops 3221356544 | bytes 7340032 | tf_op jit(solution)/shard_map/dot_general | solution.py:60
  324.2 0.0 copy-done.5
  324.2 0.2 maximum_subtract_fusion
  324.4 1.3 copy.29
  325.7 3.6 %all-to-all-start.5 = ((f32[2,256,512]{1,0,2:T(2,128)}), f32[2,256,512]{1,0,2:T(2,128)S(1)}, u32[]{:S(2)}, u32[]{:S(2)}) async-start(f32[2,256,512]{1,0,2:T(2,128)} %copy.29), calls=%async_computation.5 | async-start | bytes 2097152 | tf_op jit(solution)/shard_map/all_to_all | solution.py:95
  330.5 15.5 %all-to-all-done.5 = f32[2,256,512]{1,0,2:T(2,128)S(1)} async-done(((f32[2,256,512]{1,0,2:T(2,128)}), f32[2,256,512]{1,0,2:T(2,128)S(1)}, u32[]{:S(2)}, u32[]{:S(2)}) %all-to-all-start.5) | async-done | bytes 1048608 | tf_op jit(solution)/shard_map/all_to_all | solution.py:95
  346.0 0.1 copy.30
  346.1 0.1 copy.33
  346.2 1.6 fusion.8
  (1 shorter events, 0.0 us)
Async XLA Ops:
  6.5 148.0 %copy-start = (f32[2048]{0:T(1024)S(1)}, f32[2048]{0:T(1024)}, u32[]{:S(2)}) copy-start(f32[2048]{0:T(1024)} %param.9) | copy-start | bytes 24580
  12.1 15.4 %all-to-all-start.1 = ((f32[8,2,128,64]{2,3,1,0:T(8,128)}), f32[8,2,128,64]{2,3,1,0:T(8,128)S(1)}, u32[]{:S(2)}, u32[]{:S(2)}) async-start(f32[8,2,128,64]{2,3,1,0:T(8,128)} %copy.21), calls=%async_computation.1 | async-start | bytes 1048576 | tf_op jit(solution)/shard_map/all_to_all | solution.py:33
  27.5 12.4 %all-to-all-start = ((f32[8,2,128,64]{2,3,1,0:T(8,128)}), f32[8,2,128,64]{2,3,1,0:T(8,128)S(1)}, u32[]{:S(2)}, u32[]{:S(2)}) async-start(f32[8,2,128,64]{2,3,1,0:T(8,128)} %copy.20), calls=%async_computation | async-start | bytes 1048576 | tf_op jit(solution)/shard_map/all_to_all | solution.py:33
  39.9 33.6 %all-to-all-start.3 = ((f32[8,2,128,256]{3,2,1,0:T(8,128)}), f32[8,2,128,256]{3,2,1,0:T(8,128)S(1)}, u32[]{:S(2)}, u32[]{:S(2)}) async-start(f32[8,2,128,256]{3,2,1,0:T(8,128)} %copy.25), calls=%async_computation.3 | async-start | bytes 4194304 | tf_op jit(solution)/shard_map/all_to_all | solution.py:33
  73.5 33.9 %all-to-all-start.2 = ((f32[8,2,128,256]{3,2,1,0:T(8,128)}), f32[8,2,128,256]{3,2,1,0:T(8,128)}, u32[]{:S(2)}, u32[]{:S(2)}) async-start(f32[8,2,128,256]{3,2,1,0:T(8,128)} %copy.24), calls=%async_computation.2 | async-start | bytes 4194304 | tf_op jit(solution)/shard_map/all_to_all | solution.py:33
  77.8 226.6 %all-reduce.2.cloned.1.call-start = ((), (), s32[]{:S(2)}) async-start(), calls=%async_computation.6 | async-start | bytes 16777216 | tf_op jit(solution)/shard_map/psum | solution.py:92
  81.0 29.7 %copy-start.3 = (f32[8,2,128,256]{2,3,0,1:T(8,128)S(1)}, f32[8,2,128,256]{2,3,0,1:T(8,128)}, u32[]{:S(2)}) copy-start(f32[8,2,128,256]{2,3,0,1:T(8,128)} %copy.27) | copy-start | bytes 6291460
  113.2 11.2 %copy-start.1 = (f32[1,256,8,256]{1,3,2,0:T(8,128)}, f32[1,256,8,256]{1,3,2,0:T(8,128)S(1)}, u32[]{:S(2)}) copy-start(f32[1,256,8,256]{1,3,2,0:T(8,128)S(1)} %get-tuple-element.7) | copy-start | bytes 6291460
  143.9 0.7 copy-start.6
  143.9 10.8 %copy-start.4 = (f32[8,2,256,64]{2,3,0,1:T(8,128)S(1)}, f32[8,2,256,64]{2,3,0,1:T(8,128)}, u32[]{:S(2)}) copy-start(f32[8,2,256,64]{2,3,0,1:T(8,128)} %get-tuple-element.13) | copy-start | bytes 3145732
  304.4 4.1 %copy-start.2 = (f32[1,256,8,256]{1,3,2,0:T(8,128)S(1)}, f32[1,256,8,256]{1,3,2,0:T(8,128)}, u32[]{:S(2)}) copy-start(f32[1,256,8,256]{1,3,2,0:T(8,128)} %copy-done.1) | copy-start | bytes 6291460
  320.3 3.9 %copy-start.5 = (f32[2,256,512]{2,1,0:T(8,128)S(1)}, f32[2,256,512]{2,1,0:T(8,128)}, u32[]{:S(2)}) copy-start(f32[2,256,512]{2,1,0:T(8,128)} %copy.28) | copy-start | bytes 3145732
  325.7 20.3 %all-to-all-start.5 = ((f32[2,256,512]{1,0,2:T(2,128)}), f32[2,256,512]{1,0,2:T(2,128)S(1)}, u32[]{:S(2)}, u32[]{:S(2)}) async-start(f32[2,256,512]{1,0,2:T(2,128)} %copy.29), calls=%async_computation.5 | async-start | bytes 2097152 | tf_op jit(solution)/shard_map/all_to_all | solution.py:95
Sparse Core Ops, SparseCore 0:
  144.1 160.2 all-reduce.1
where the time goes:
time: 359 us; the launch traced here: 355 us
  waiting for transfers between devices  229 us (64%)
  matrix products  42.2 us (12%)
  local copies, waits for them, and re-layouts  21.8 us (6%)
  starting transfers between devices  20.9 us (6%)
  between operations  16.2 us (5%)
  other arithmetic  15.9 us (4%)
  blocking collectives  8.52 us (2%)
    psum x1, waiting for transfers between devices, per_device(): margin = lax.psum(margin_of(row_waves, row_columns), ('ga', 'ba'))  148 us
    all_to_all x4, waiting for transfers between devices, cut_exchange(): lax.all_to_all(slab, axis, split_axis=0, concat_axis=0, tiled=True)  65.3 us
    dot_general x4, matrix products, tdot(): lax.dot_general(left, right, (((0,), (0,)), ((), ())), precision=lax.Prec...  26.5 us
    all_to_all x4, starting transfers between devices, cut_exchange(): lax.all_to_all(slab, axis, split_axis=0, concat_axis=0, tiled=True)  17.3 us
    dot_general x5, matrix products, mdot(): jnp.dot(left, right, precision=lax.Precision.HIGHEST, preferred_element_t...  15.8 us
    all_to_all x1, waiting for transfers between devices, per_device(): lax.all_to_all(row_result, 'ba', split_axis=2, concat_axis=1, tiled=True)  15.5 us
    split x6, local copies, waits for them, and re-layouts, cut_exchange(): jnp.split(blocks, edges_of(blocks.shape[split_at], pieces), axis=split_at)  10.5 us
    all_to_all x1, blocking collectives, from_everyone(): lax.all_to_all(jnp.broadcast_to(value[None], (count, *value.shape)), axis...  8.52 us
  transfers between devices with their start and end apart: 6, of which 6 were waited for; matrix products, arithmetic and copies ran while one was open for 4% of the time, Pallas kernels for 0%

commit v1 on v0

--- a/solution.py
+++ b/solution.py
@@ -89,7 +89,7 @@
     )
     all_panels = gather_directly(panel_band, "ba", 0)
     full_weight = weights_for(band_weight, all_panels)
-    margin = lax.psum(margin_of(row_waves, row_columns), ("ga", "ba"))
+    margin = lax.psum(lax.psum(margin_of(row_waves, row_columns), "ba"), "ga")
     weighted = margin * full_weight[None, :, None]
     row_result = row_columns - correct_with(row_waves, weighted)
     result = lax.all_to_all(row_result, "ba", split_axis=2, concat_axis=1, tiled=True)

time: 359 us -> 747 us (2.08)
  waiting for transfers between devices: 229 us -> 611 us
    psum x1 -> x2, waiting for transfers between devices: 148 us -> 529 us  [per_device(): margin = lax.psum(lax.psum(margin_of(row_waves, row_columns), 'ba'), 'ga')]
  transfers between devices with their start and end apart: 6 -> 7, of which waited for: 6 -> 7; matrix products, arithmetic and copies ran while one was open for 4% -> 2% of each run, Pallas kernels for 0% -> 0%
where the time goes in v1:
time: 747 us; the launch traced here: 743 us
  waiting for transfers between devices  611 us (82%)
  matrix products  42.3 us (6%)
  local copies, waits for them, and re-layouts  21.8 us (3%)
  starting transfers between devices  21.6 us (3%)
  between operations  16.2 us (2%)
  other arithmetic  15.9 us (2%)
  blocking collectives  14.1 us (2%)
    psum x2, waiting for transfers between devices, per_device(): margin = lax.psum(lax.psum(margin_of(row_waves, row_columns), 'ba'), 'ga')  529 us
    all_to_all x4, waiting for transfers between devices, cut_exchange(): lax.all_to_all(slab, axis, split_axis=0, concat_axis=0, tiled=True)  65.3 us
    dot_general x4, matrix products, tdot(): lax.dot_general(left, right, (((0,), (0,)), ((), ())), precision=lax.Prec...  26.5 us
    all_to_all x4, starting transfers between devices, cut_exchange(): lax.all_to_all(slab, axis, split_axis=0, concat_axis=0, tiled=True)  17.3 us
    all_to_all x1, waiting for transfers between devices, per_device(): lax.all_to_all(row_result, 'ba', split_axis=2, concat_axis=1, tiled=True)  16.3 us
    dot_general x5, matrix products, mdot(): jnp.dot(left, right, precision=lax.Precision.HIGHEST, preferred_element_t...  15.8 us
  transfers between devices with their start and end apart: 7, of which 7 were waited for; matrix products, arithmetic and copies ran while one was open for 2% of the time, Pallas kernels for 0%

profile of v1, /device:TPU:2, one launch (start us, length us, event | category | flops | bytes accessed | tf_op | source)
XLA Modules:
  0.0 742.8 jit_solution(13227554287532873247)
XLA Ops:
  6.5 0.0 copy-start
  6.5 1.2 dynamic_slice.6
  8.9 1.8 fusion.9
  10.8 0.3 copy.34
  11.1 0.1 fusion.15
  11.2 0.9 copy.21
  12.1 5.8 all-to-all-start.1
  17.9 0.9 copy.20
  18.8 8.7 %all-to-all-done.1 = f32[8,2,128,64]{2,3,1,0:T(8,128)S(1)} async-done(((f32[8,2,128,64]{2,3,1,0:T(8,128)}), f32[8,2,128,64]{2,3,1,0:T(8,128)S(1)}, u32[]{:S(2)}, u32[]{:S(2)}) %all-to-all-start.1) | async-done | bytes 524320 | tf_op jit(solution)/shard_map/all_to_all | solution.py:33
  27.5 3.5 all-to-all-start
  31.0 4.0 fusion.13
  34.9 1.6 copy.25
  36.5 3.4 all-to-all-done
  39.9 3.6 all-to-all-start.3
  43.5 3.1 copy.24
  46.6 26.9 %all-to-all-done.3 = f32[8,2,128,256]{3,2,1,0:T(8,128)S(1)} async-done(((f32[8,2,128,256]{3,2,1,0:T(8,128)}), f32[8,2,128,256]{3,2,1,0:T(8,128)S(1)}, u32[]{:S(2)}, u32[]{:S(2)}) %all-to-all-start.3) | async-done | bytes 2097184 | tf_op jit(solution)/shard_map/all_to_all | solution.py:33
  73.5 4.3 all-to-all-start.2
  77.8 0.0 all-reduce.3.cloned.1.call-start
  77.9 1.1 copy_bitcast_fusion
  79.0 0.1 fusion.14
  79.1 1.9 copy.27
  81.0 0.0 copy-start.3
  81.0 26.4 %all-to-all-done.2 = f32[8,2,128,256]{3,2,1,0:T(8,128)} async-done(((f32[8,2,128,256]{3,2,1,0:T(8,128)}), f32[8,2,128,256]{3,2,1,0:T(8,128)}, u32[]{:S(2)}, u32[]{:S(2)}) %all-to-all-start.2) | async-done | bytes 2097184 | tf_op jit(solution)/shard_map/all_to_all | solution.py:33
  107.4 3.3 copy.26
  110.7 0.0 copy-done.3
  110.7 2.1 maximum_bitcast_fusion
  112.8 0.4 fusion.12
  113.2 0.0 copy-start.1
  113.2 3.7 fusion.17
  116.9 3.7 fusion.16
  120.7 3.8 subtract_bitcast_fusion
  124.4 0.0 copy-done.1
  124.4 15.3 %add_bitcast_fusion = f32[1,2048,512]{2,1,0:T(8,128)S(1)} fusion(f32[2048,512]{1,0:T(8,128)S(1)} %fusion.16, f32[256,2048]{0,1:T(8,128)S(1)} %bitcast.73, f32[256,512]{0,1:T(8,128)S(1)} %bitcast.77), kind=kOutput, calls=%fused_computation.6 | convolution fusion | flops 3222274048 | bytes 11010048 | tf_op jit(solution)/shard_map/dot_general | solution.py:50
  139.8 4.2 pad_maximum_fusion
  144.0 0.0 all-reduce.3.cloned.1.call-update
  144.0 0.0 all-reduce.5.cloned.1.call-start
  144.1 339.0 %all-reduce.3.cloned.1.call-done = f32[2,2048,512]{2,1,0:T(8,128)} async-done(((f32[2,2048,512]{2,1,0:T(8,128)}), f32[2,2048,512]{2,1,0:T(8,128)}) %all-reduce.3.cloned.1.call-update) | async-done | bytes 8388624 | tf_op jit(solution)/shard_map/psum | solution.py:92
  483.1 0.0 copy-start.6
  483.1 0.0 all-reduce.5.cloned.1.call-update
  483.1 0.6 copy-done.6
  483.8 14.1 %all_to_all.44 = s32[8,1,2]{2,1,0:T(1,128)S(1)} all-to-all(s32[8,1,2]{2,1,0:T(1,128)S(1)} %broadcast_in_dim.2), channel_id=1, replica_groups=mesh['ga'=16,'ba'=8] {'ba'}, dimensions={0} | all-to-all | bytes 128 | tf_op jit(solution)/shard_map/all_to_all | solution.py:39
  497.9 0.6 broadcast.7
  498.4 0.7 reduce.3
  499.2 0.1 eq.17
  499.2 0.0 copy-done
  499.2 0.2 convolution_bitcast_fusion
  499.4 0.0 copy-done.4
  499.4 1.3 copy.28
  500.8 190.2 %all-reduce.5.cloned.1.call-done = f32[2,2048,512]{2,1,0:T(8,128)} async-done(((f32[2,2048,512]{2,1,0:T(8,128)}), f32[2,2048,512]{2,1,0:T(8,128)}) %all-reduce.5.cloned.1.call-update) | async-done | bytes 8388624 | tf_op jit(solution)/shard_map/psum | solution.py:92
  690.9 4.1 broadcast_multiply_fusion
  695.1 0.0 copy-done.2
  695.1 3.8 fusion
  698.9 3.9 fusion.1
  702.8 4.1 fusion.7
  706.8 0.0 copy-start.5
  706.9 3.8 fusion.5
  710.7 0.0 copy-done.5
  710.7 0.2 maximum_subtract_fusion
  710.9 1.3 copy.29
  712.2 4.3 all-to-all-start.5
  717.7 16.3 %all-to-all-done.5 = f32[2,256,512]{1,0,2:T(2,128)S(1)} async-done(((f32[2,256,512]{1,0,2:T(2,128)}), f32[2,256,512]{1,0,2:T(2,128)S(1)}, u32[]{:S(2)}, u32[]{:S(2)}) %all-to-all-start.5) | async-done | bytes 1048608 | tf_op jit(solution)/shard_map/all_to_all | solution.py:95
  734.0 0.1 copy.30
  734.0 0.1 copy.33
  734.2 1.6 fusion.8
  (3 shorter events, 0.0 us)
Async XLA Ops:
  6.5 492.7 %copy-start = (f32[2048]{0:T(1024)S(1)}, f32[2048]{0:T(1024)}, u32[]{:S(2)}) copy-start(f32[2048]{0:T(1024)} %param.9) | copy-start | bytes 24580
  12.1 15.4 %all-to-all-start.1 = ((f32[8,2,128,64]{2,3,1,0:T(8,128)}), f32[8,2,128,64]{2,3,1,0:T(8,128)S(1)}, u32[]{:S(2)}, u32[]{:S(2)}) async-start(f32[8,2,128,64]{2,3,1,0:T(8,128)} %copy.21), calls=%async_computation.1 | async-start | bytes 1048576 | tf_op jit(solution)/shard_map/all_to_all | solution.py:33
  27.5 12.4 %all-to-all-start = ((f32[8,2,128,64]{2,3,1,0:T(8,128)}), f32[8,2,128,64]{2,3,1,0:T(8,128)S(1)}, u32[]{:S(2)}, u32[]{:S(2)}) async-start(f32[8,2,128,64]{2,3,1,0:T(8,128)} %copy.20), calls=%async_computation | async-start | bytes 1048576 | tf_op jit(solution)/shard_map/all_to_all | solution.py:33
  39.9 33.6 %all-to-all-start.3 = ((f32[8,2,128,256]{3,2,1,0:T(8,128)}), f32[8,2,128,256]{3,2,1,0:T(8,128)S(1)}, u32[]{:S(2)}, u32[]{:S(2)}) async-start(f32[8,2,128,256]{3,2,1,0:T(8,128)} %copy.25), calls=%async_computation.3 | async-start | bytes 4194304 | tf_op jit(solution)/shard_map/all_to_all | solution.py:33
  73.5 33.9 %all-to-all-start.2 = ((f32[8,2,128,256]{3,2,1,0:T(8,128)}), f32[8,2,128,256]{3,2,1,0:T(8,128)}, u32[]{:S(2)}, u32[]{:S(2)}) async-start(f32[8,2,128,256]{3,2,1,0:T(8,128)} %copy.24), calls=%async_computation.2 | async-start | bytes 4194304 | tf_op jit(solution)/shard_map/all_to_all | solution.py:33
  77.8 405.3 %all-reduce.3.cloned.1.call-start = ((), (), s32[]{:S(2)}) async-start(), calls=%async_computation.6 | async-start | bytes 16777216 | tf_op jit(solution)/shard_map/psum | solution.py:92
  81.0 29.7 %copy-start.3 = (f32[8,2,128,256]{2,3,0,1:T(8,128)S(1)}, f32[8,2,128,256]{2,3,0,1:T(8,128)}, u32[]{:S(2)}) copy-start(f32[8,2,128,256]{2,3,0,1:T(8,128)} %copy.27) | copy-start | bytes 6291460
  113.2 11.2 %copy-start.1 = (f32[1,256,8,256]{1,3,2,0:T(8,128)}, f32[1,256,8,256]{1,3,2,0:T(8,128)S(1)}, u32[]{:S(2)}) copy-start(f32[1,256,8,256]{1,3,2,0:T(8,128)S(1)} %get-tuple-element.7) | copy-start | bytes 6291460
  144.0 546.9 %all-reduce.5.cloned.1.call-start = ((), (), s32[]{:S(2)}) async-start(), calls=%async_computation.7 | async-start | bytes 16777216 | tf_op jit(solution)/shard_map/psum | solution.py:92
  483.1 0.7 copy-start.6
  483.1 16.3 %copy-start.4 = (f32[8,2,256,64]{2,3,0,1:T(8,128)S(1)}, f32[8,2,256,64]{2,3,0,1:T(8,128)}, u32[]{:S(2)}) copy-start(f32[8,2,256,64]{2,3,0,1:T(8,128)} %get-tuple-element.13) | copy-start | bytes 3145732
  690.9 4.1 copy-start.2
  706.8 3.9 copy-start.5
  712.2 21.7 %all-to-all-start.5 = ((f32[2,256,512]{1,0,2:T(2,128)}), f32[2,256,512]{1,0,2:T(2,128)S(1)}, u32[]{:S(2)}, u32[]{:S(2)}) async-start(f32[2,256,512]{1,0,2:T(2,128)} %copy.29), calls=%async_computation.5 | async-start | bytes 2097152 | tf_op jit(solution)/shard_map/all_to_all | solution.py:95
Sparse Core Ops, SparseCore 0:
  144.1 338.9 all-reduce.2
  485.6 205.2 all-reduce.4
